TPU v7x, 32 devices: a whole 2x2x4 slice. The times are simulated.
32 devices in a mesh: row: 8 (over z, y), col: 4 (over x, core).
Axes of the slice: x: 2, y: 2, z: 4, core: 2. Of those that a mesh axis runs over, the one named last changes fastest.
Arguments:
- matrix: float32 [4, 8, 512, 8, 4, 512], P(None, 'row', None, None, 'col'), may hold values from -30 to 30, as said below
Outputs:
- factored: float32 [4, 8, 512, 8, 4, 512], P(None, 'row', None, None, 'col')
Inputs may be any that keep to these rules, and one draw needn't show every extreme that they name: matrix is symmetric, positive definite and well conditioned.
All inputs are finite; a program needn't handle non-finite values.
Results may differ from a plain program's by a relative error of at most 0.00013.
Values sent between devices are 32-bit elements; how exact they have to be, the bound alone decides.
A program may use at most 192 MiB of HBM per device.

v0:
```python
import jax
import jax.numpy as jnp
from jax import lax
from jax.sharding import PartitionSpec as P

NB = 512
STEPS = 2


def spread(value, axis, source):
    kept = jnp.where(lax.axis_index(axis) == source, value, 0).astype(value.dtype)
    return lax.psum(kept, axis)


def trailing_product(column_panel, transposed):
    return jnp.einsum(
        "tan,sbn->tasb",
        column_panel,
        transposed,
        precision=lax.Precision.HIGHEST,
        preferred_element_type=jnp.float32,
    )


def shards(matrix):
    local_rows = matrix.shape[0]
    local_cols = matrix.shape[3]
    blocks = matrix.reshape(local_rows, NB, local_cols, NB)
    row_count = lax.axis_size("row")
    column_count = lax.axis_size("col")
    group_size = row_count // column_count
    row_place = lax.axis_index("row")
    column_place = lax.axis_index("col")
    tile_rows = jnp.arange(local_rows, dtype=jnp.int32) * row_count + row_place
    tile_columns = jnp.arange(local_cols, dtype=jnp.int32) * column_count + column_place
    anchor = jnp.int32(0)
    for step in range(STEPS):
        root_row = step % row_count
        factor_local_row = step // row_count
        root_col = step % column_count
        factor_local_col = step // column_count
        corner = blocks[factor_local_row, :, factor_local_col, :]
        owner = (row_place == root_row) & (column_place == root_col)
        identity = jnp.eye(NB, dtype=jnp.float32)
        chosen = jnp.where(owner, corner, identity)
        factor_local = jnp.linalg.cholesky(chosen)
        factor_diag_block = spread(factor_local, "row", root_row)
        source = blocks[:, :, factor_local_col, :]
        solved = jax.scipy.linalg.solve_triangular(
            factor_diag_block, source.reshape(local_rows * NB, NB).T, lower=True
        ).T
        solved = solved.reshape(local_rows, NB, NB)
        panel_local = jnp.where((tile_rows > step)[:, None, None], solved, 0.0)
        factor_column_panel = spread(panel_local, "col", root_col)
        empty = jnp.zeros((local_rows, group_size, NB, NB), jnp.float32)
        slot_index = row_place // column_count
        holder = row_place % column_count == column_place
        contribution = jnp.where(holder, factor_column_panel, 0.0)
        filled = lax.dynamic_update_slice(
            empty, contribution[:, None], (anchor, slot_index, anchor, anchor)
        )
        gathered = lax.psum(filled, "row")
        transposed = gathered.reshape(local_cols, NB, NB)
        diag_block, column_panel, transposed = (factor_diag_block, factor_column_panel, transposed)
        write_blocks = blocks
        local_row = step // row_count
        local_col = step // column_count
        column_now = write_blocks[:, :, local_col, :]
        owns_col = column_place == step % column_count
        row_after = (tile_rows > step)[:, None, None]
        row_hit = (tile_rows == step)[:, None, None]
        new_column = jnp.where(
            row_after, column_panel, jnp.where(row_hit, diag_block[None], column_now)
        )
        new_column = jnp.where(owns_col, new_column, column_now)
        write_blocks = write_blocks.at[:, :, local_col, :].set(new_column)
        row_now = write_blocks[local_row]
        owns_row = row_place == step % row_count
        zero_cols = (tile_columns > step)[None, :, None]
        new_row = jnp.where(owns_row & zero_cols, 0.0, row_now)
        blocks = write_blocks.at[local_row].set(new_row)
        blocks = blocks - trailing_product(column_panel, transposed)
    return blocks.reshape(matrix.shape)


def solution(mesh):
    in_specs = (P(None, "row", None, None, "col", None),)
    out_specs = P(None, "row", None, None, "col", None)
    return jax.shard_map(shards, mesh=mesh, in_specs=in_specs, out_specs=out_specs, check_vma=False)
```

profile of v0, /device:TPU:0, one launch (start us, length us, event | category | flops | bytes accessed | tf_op | source)
XLA Modules:
  0.0 1563.9 jit_solution(13661579687502120736)
XLA Ops:
  6.5 78.2 %copy.17 = f32[4,1,512,8,1,512]{2,5,3,0,4,1:T(8,128)} copy(f32[4,1,512,8,1,512]{5,4,3,2,1,0:T(1,128)} %param.12) | data formatting | bytes 67108864 | tf_op args[0]
  86.4 1.5 fusion.39
  87.9 11.7 cholesky.286
  99.7 9.8 custom-call.27
  110.3 11.7 cholesky.305
  122.0 10.0 custom-call.28
  132.7 11.7 cholesky.326
  145.2 9.8 custom-call.29
  155.6 11.7 cholesky.343
  182.8 78.7 %copy.42 = f32[4,1,512,8,1,512]{2,5,0,3,1,4:T(8,128)} copy(f32[4,1,512,8,1,512]{5,4,3,2,1,0:T(1,128)} %param.12) | data formatting | bytes 67108864 | tf_op jit(solution)/shard_map/reshape | solution.py:28
  261.6 4.6 slice.220
  266.2 5.3 copy.20
  271.5 1.3 fusion.42
  272.9 7.6 while.8
  280.5 39.3 %custom-call.30 = f32[4,128,128]{1,2,0:T(8,128)S(1)} custom-call(f32[4,128,128]{2,1,0:T(8,128)S(1)} %get-tuple-element.69), custom_call_target="InvertDiagBlocksLowerTriangular" | custom-call | tf_op jit(solution)/shard_map/jit(_solve_triangular)/triangular_solve | solution.py:49
  319.8 2.4 fusion.36
  322.3 3.0 convolution_subtract_fusion.4
  326.4 3.5 convolution_subtract_fusion.2
  331.0 5.7 fusion.25
  337.8 2.4 maximum_bitcast_fusion
  340.3 5.4 copy.21
  345.7 5.2 copy.22
  350.9 4.9 select_select_fusion.1
  355.9 88.4 %all-reduce.10.cloned.1.call-done = f32[4,512,512]{1,2,0:T(8,128)} async-done(((f32[4,512,512]{1,2,0:T(8,128)}), f32[4,512,512]{1,2,0:T(8,128)}) %all-reduce.10.cloned.1.call-update) | async-done | bytes 4194320 | tf_op jit(solution)/shard_map/psum | solution.py:12
  444.2 4.6 select_bitcast_fusion.1
  448.9 5.3 copy.25
  454.1 4.3 broadcast.312.clone
  458.4 2.4 constant_dynamic-update-slice_fusion.3
  462.3 6.8 bitcast_dynamic-update-slice_fusion.2
  469.2 8.3 fusion.1
  477.5 253.1 %all-reduce.12.cloned.1.call-done = f32[8,512,512]{2,1,0:T(8,128)} async-done(((f32[8,512,512]{2,1,0:T(8,128)}), f32[8,512,512]{2,1,0:T(8,128)}) %all-reduce.12.cloned.1.call-update) | async-done | bytes 8388624 | tf_op jit(solution)/shard_map/psum | solution.py:62
  730.6 63.0 %convolution_subtract_fusion = f32[4,512,8,512]{1,3,2,0:T(8,128)} fusion(f32[4,512,8,512]{1,3,2,0:T(8,128)} %fusion.1, f32[8,512,512]{2,1,0:T(8,128)} %all-reduce.12.cloned.1.call-done, f32[4,512,512]{1,2,0:T(8,128)} %all-reduce.10.cloned.1.call-done), kind=kOutput, calls=%fused_computation.5 | convolution fusion | flops 51547996160 | bytes 79691776 | tf_op jit(solution)/shard_map/tan,sbn->tasb/dot_general | solution.py:16
  793.5 1.3 convert_select_fusion
  795.2 1.5 fusion.38
  796.7 11.7 cholesky.358
  808.6 9.8 custom-call.31
  819.1 11.7 cholesky.377
  832.2 10.2 custom-call.32
  843.0 11.7 cholesky.398
  855.5 9.8 custom-call.33
  865.9 11.7 cholesky.415
  882.3 6.8 fusion.84
  889.0 5.2 copy.30
  894.3 65.6 %all-reduce.14.cloned.1.call-done = f32[512,512]{1,0:T(8,128)} async-done(((f32[512,512]{1,0:T(8,128)}), f32[512,512]{1,0:T(8,128)}) %all-reduce.14.cloned.1.call-update) | async-done | bytes 1048592 | tf_op jit(solution)/shard_map/psum | solution.py:12
  961.2 7.8 while.9
  969.0 39.3 %custom-call.34 = f32[4,128,128]{1,2,0:T(8,128)S(1)} custom-call(f32[4,128,128]{2,1,0:T(8,128)S(1)} %get-tuple-element.70), custom_call_target="InvertDiagBlocksLowerTriangular" | custom-call | tf_op jit(solution)/shard_map/jit(_solve_triangular)/triangular_solve | solution.py:49
  1008.4 2.4 fusion.34
  1010.8 3.0 convolution_subtract_fusion.3
  1015.0 3.5 convolution_subtract_fusion.1
  1019.6 5.6 fusion.22
  1026.2 2.5 maximum_bitcast_fusion.1
  1028.7 5.3 copy.31
  1034.0 5.2 copy.32
  1039.3 4.9 select_select_fusion
  1044.2 85.2 %all-reduce.16.cloned.1.call-done = f32[4,512,512]{1,2,0:T(8,128)} async-done(((f32[4,512,512]{1,2,0:T(8,128)}), f32[4,512,512]{1,2,0:T(8,128)}) %all-reduce.16.cloned.1.call-update) | async-done | bytes 4194320 | tf_op jit(solution)/shard_map/psum | solution.py:12
  1129.4 4.6 select_bitcast_fusion
  1134.0 5.3 copy.34
  1139.3 4.3 broadcast.312
  1143.6 2.4 constant_dynamic-update-slice_fusion.2
  1147.6 6.8 fusion.6
  1154.4 8.3 fusion
  1162.7 253.0 %all-reduce.18.cloned.1.call-done = f32[8,512,512]{2,1,0:T(8,128)} async-done(((f32[8,512,512]{2,1,0:T(8,128)}), f32[8,512,512]{2,1,0:T(8,128)}) %all-reduce.18.cloned.1.call-update) | async-done | bytes 8388624 | tf_op jit(solution)/shard_map/psum | solution.py:62
  1415.8 62.8 %subtract_bitcast_fusion = f32[4,1,512,8,1,512]{2,5,3,0,4,1:T(8,128)} fusion(f32[4,512,8,512]{1,3,2,0:T(8,128)} %fusion, f32[8,512,512]{2,1,0:T(8,128)} %all-reduce.18.cloned.1.call-done, f32[4,512,512]{1,2,0:T(8,128)} %all-reduce.16.cloned.1.call-done), kind=kOutput, calls=%fused_computation.4 | convolution fusion | flops 51547996160 | bytes 79691776 | tf_op jit(solution)/shard_map/tan,sbn->tasb/dot_general | solution.py:16
  1478.5 78.2 %copy.37 = f32[4,1,512,8,1,512]{5,4,3,2,1,0:T(1,128)} copy(f32[4,1,512,8,1,512]{2,5,3,0,4,1:T(8,128)} %subtract_bitcast_fusion) | data formatting | bytes 67108864 | tf_op jit(solution)/shard_map/reshape | solution.py:83
  (108 shorter events, 39.8 us)
Async XLA Ops:
  6.5 264.9 %all-reduce.8.cloned.1.call-start = ((), (), s32[]{:S(2)}) async-start(), calls=%async_computation | async-start | bytes 2097152 | tf_op jit(solution)/shard_map/psum | solution.py:12
  182.8 261.4 %all-reduce.10.cloned.1.call-start = ((), (), s32[]{:S(2)}) async-start(), calls=%async_computation.1 | async-start | bytes 8388608 | tf_op jit(solution)/shard_map/psum | solution.py:12
  319.8 6.6 copy-start.2
  355.8 374.8 %all-reduce.12.cloned.1.call-start = ((), (), s32[]{:S(2)}) async-start(), calls=%async_computation.2 | async-start | bytes 16777216 | tf_op jit(solution)/shard_map/psum | solution.py:62
  454.1 4.3 copy-start.1
  460.8 1.2 copy-start.4
  460.8 499.0 %all-reduce.14.cloned.1.call-start = ((), (), s32[]{:S(2)}) async-start(), calls=%async_computation.3 | async-start | bytes 2097152 | tf_op jit(solution)/shard_map/psum | solution.py:12
  882.2 247.2 %all-reduce.16.cloned.1.call-start = ((), (), s32[]{:S(2)}) async-start(), calls=%async_computation.4 | async-start | bytes 8388608 | tf_op jit(solution)/shard_map/psum | solution.py:12
  1008.4 6.6 copy-start.3
  1044.2 371.6 %all-reduce.18.cloned.1.call-start = ((), (), s32[]{:S(2)}) async-start(), calls=%async_computation.5 | async-start | bytes 16777216 | tf_op jit(solution)/shard_map/psum | solution.py:62
  1139.3 4.3 copy-start
  1146.0 1.2 copy-start.5
Sparse Core Ops, SparseCore 0:
  182.9 81.0 all-reduce.7
  355.9 88.2 all-reduce.9
  460.9 269.6 all-reduce.11
  882.3 77.4 all-reduce.13
  1044.3 85.0 all-reduce.15
  1146.1 269.5 all-reduce.17
where the time goes:
time: 1580 us; the launch traced here: 1560 us
  waiting for transfers between devices  745 us (47%)
  local copies, waits for them, and re-layouts  321 us (20%)
  other arithmetic  302 us (19%)
  matrix products  165 us (10%)
  between operations  30 us (2%)
    psum x2, waiting for transfers between devices, shards(): gathered = lax.psum(filled, 'row')  506 us
    psum x4, waiting for transfers between devices, spread(): return lax.psum(kept, axis)  239 us
    another operation x29, other arithmetic, shards(): factor_local = jnp.linalg.cholesky(chosen)  158 us
    dot_general x2, matrix products, trailing_product(): jnp.einsum('tan,sbn->tasb', column_panel, transposed, precision=lax.Preci...  126 us
    another operation x5, other arithmetic, shards(): jax.scipy.linalg.solve_triangular(factor_diag_block, source.reshape(local...  81.3 us
    unnamed x13, local copies, waits for them, and re-layouts  80.5 us
    reshape x1, local copies, waits for them, and re-layouts, shards(): blocks = matrix.reshape(local_rows, NB, local_cols, NB)  78.7 us
    reshape x1, local copies, waits for them, and re-layouts, shards(): return blocks.reshape(matrix.shape)  78.2 us
  transfers between devices with their start and end apart: 6, of which 5 were waited for; matrix products, arithmetic and copies ran while one was open for 8% of the time, Pallas kernels for 0%

commit v1 on v0

--- a/solution.py
+++ b/solution.py
@@ -5,6 +5,15 @@
 
 NB = 512
 STEPS = 2
+
+
+def doubling_sum(x, axis):
+    size = lax.axis_size(axis)
+    summed, stride = (x, 1)
+    while stride < size:
+        summed = summed + lax.ppermute(summed, axis, [(i, i ^ stride) for i in range(size)])
+        stride = 2 * stride
+    return summed
 
 
 def spread(value, axis, source):
@@ -59,7 +68,7 @@
         filled = lax.dynamic_update_slice(
             empty, contribution[:, None], (anchor, slot_index, anchor, anchor)
         )
-        gathered = lax.psum(filled, "row")
+        gathered = doubling_sum(filled, "row")
         transposed = gathered.reshape(local_cols, NB, NB)
         diag_block, column_panel, transposed = (factor_diag_block, factor_column_panel, transposed)
         write_blocks = blocks

time: 1580 us -> 2530 us (1.60)
  waiting for transfers between devices: 745 us -> 1650 us
  other arithmetic: 302 us -> 341 us
    ppermute x0 -> x6, waiting for transfers between devices: none -> 1410 us  [doubling_sum(): lax.ppermute(summed, axis, [(i, i ^ stride) for i in range(size)])]
    psum x2 -> x0, waiting for transfers between devices: 506 us -> none  [shards(): gathered = lax.psum(filled, 'row')]
    add x0 -> x6, other arithmetic: none -> 46.9 us  [doubling_sum(): summed + lax.ppermute(summed, axis, [(i, i ^ stride) for i in range(size)])]
    unnamed x13 -> x17, local copies, waits for them, and re-layouts: 80.5 us -> 86.9 us
  transfers between devices with their start and end apart: 6 -> 10, of which waited for: 5 -> 9; matrix products, arithmetic and copies ran while one was open for 8% -> 5% of each run, Pallas kernels for 0% -> 0%
where the time goes in v1:
time: 2530 us; the launch traced here: 2510 us
  waiting for transfers between devices  1650 us (65%)
  other arithmetic  341 us (13%)
  local copies, waits for them, and re-layouts  326 us (13%)
  matrix products  166 us (7%)
    ppermute x6, waiting for transfers between devices, doubling_sum(): lax.ppermute(summed, axis, [(i, i ^ stride) for i in range(size)])  1410 us
    psum x4, waiting for transfers between devices, spread(): return lax.psum(kept, axis)  241 us
    another operation x29, other arithmetic, shards(): factor_local = jnp.linalg.cholesky(chosen)  158 us
    dot_general x2, matrix products, trailing_product(): jnp.einsum('tan,sbn->tasb', column_panel, transposed, precision=lax.Preci...  126 us
    unnamed x17, local copies, waits for them, and re-layouts  86.9 us
    another operation x5, other arithmetic, shards(): jax.scipy.linalg.solve_triangular(factor_diag_block, source.reshape(local...  81.3 us
    reshape x1, local copies, waits for them, and re-layouts, shards(): blocks = matrix.reshape(local_rows, NB, local_cols, NB)  78.7 us
    reshape x1, local copies, waits for them, and re-layouts, shards(): return blocks.reshape(matrix.shape)  78.2 us
  transfers between devices with their start and end apart: 10, of which 9 were waited for; matrix products, arithmetic and copies ran while one was open for 5% of the time, Pallas kernels for 0%

profile of v1, /device:TPU:0, one launch (start us, length us, event | category | flops | bytes accessed | tf_op | source)
XLA Modules:
  0.0 2510.5 jit_solution(17131408131632243650)
XLA Ops:
  6.5 78.2 %copy.15 = f32[4,1,512,8,1,512]{2,5,3,0,4,1:T(8,128)} copy(f32[4,1,512,8,1,512]{5,4,3,2,1,0:T(1,128)} %param.12) | data formatting | bytes 67108864 | tf_op args[0]
  87.9 11.7 cholesky.286
  99.8 9.8 custom-call.27
  110.3 11.7 cholesky.305
  122.0 10.2 custom-call.28
  133.0 11.7 cholesky.326
  144.7 9.8 custom-call.29
  155.1 11.7 cholesky.343
  172.8 78.7 %copy.40 = f32[4,1,512,8,1,512]{2,5,0,3,1,4:T(8,128)} copy(f32[4,1,512,8,1,512]{5,4,3,2,1,0:T(1,128)} %param.12) | data formatting | bytes 67108864 | tf_op jit(solution)/shard_map/reshape | solution.py:37
  251.5 4.6 slice.220
  256.1 5.3 copy.18
  262.8 7.6 while.8
  270.4 39.3 %custom-call.30 = f32[4,128,128]{1,2,0:T(8,128)S(1)} custom-call(f32[4,128,128]{2,1,0:T(8,128)S(1)} %get-tuple-element.69), custom_call_target="InvertDiagBlocksLowerTriangular" | custom-call | tf_op jit(solution)/shard_map/jit(_solve_triangular)/triangular_solve | solution.py:58
  309.8 2.4 fusion.36
  312.2 3.0 convolution_subtract_fusion.4
  316.3 3.5 convolution_subtract_fusion.2
  321.0 5.7 fusion.25
  327.8 2.4 maximum_bitcast_fusion
  330.2 5.4 copy.19
  335.6 5.2 copy.20
  340.9 4.9 select_select_fusion.1
  345.8 88.4 %all-reduce.8.cloned.1.call-done = f32[4,512,512]{1,2,0:T(8,128)} async-done(((f32[4,512,512]{1,2,0:T(8,128)}), f32[4,512,512]{1,2,0:T(8,128)}) %all-reduce.8.cloned.1.call-update) | async-done | bytes 4194320 | tf_op jit(solution)/shard_map/psum | solution.py:21
  438.5 180.4 %collective-permute-done = f32[4,2,512,512]{2,3,0,1:T(8,128)S(1)} collective-permute-done((f32[4,2,512,512]{2,3,0,1:T(8,128)S(1)}, f32[4,2,512,512]{2,3,0,1:T(8,128)S(1)}, u32[]{:S(2)}, u32[]{:S(2)}) %collective-permute-start) | collective-permute-done | bytes 8388640 | tf_op jit(solution)/shard_map/ppermute | solution.py:14
  620.2 3.2 copy-done.3
  624.9 179.6 %collective-permute-done.1 = f32[4,2,512,512]{2,3,0,1:T(8,128)} collective-permute-done((f32[4,2,512,512]{2,3,0,1:T(8,128)S(1)}, f32[4,2,512,512]{2,3,0,1:T(8,128)}, u32[]{:S(2)}, u32[]{:S(2)}) %collective-permute-start.1) | collective-permute-done | bytes 8388640 | tf_op jit(solution)/shard_map/ppermute | solution.py:14
  804.5 11.1 add.117
  818.4 6.8 bitcast_dynamic-update-slice_fusion.2
  825.2 8.3 fusion.1
  833.5 343.2 %collective-permute-done.2 = f32[4,2,512,512]{2,3,0,1:T(8,128)} collective-permute-done((f32[4,2,512,512]{2,3,0,1:T(8,128)}, f32[4,2,512,512]{2,3,0,1:T(8,128)}, u32[]{:S(2)}, u32[]{:S(2)}) %collective-permute-start.2) | collective-permute-done | bytes 8388640 | tf_op jit(solution)/shard_map/ppermute | solution.py:14
  1176.7 11.1 add.118
  1187.8 10.0 copy.23
  1197.8 63.0 %convolution_subtract_fusion = f32[4,512,8,512]{1,3,2,0:T(8,128)} fusion(f32[4,512,8,512]{1,3,2,0:T(8,128)} %fusion.1, f32[8,512,512,1]{2,1,0,3:T(8,128)} %bitcast.188, f32[4,512,512]{1,2,0:T(8,128)} %all-reduce.8.cloned.1.call-done), kind=kOutput, calls=%fused_computation.5 | convolution fusion | flops 51547996160 | bytes 79691776 | tf_op jit(solution)/shard_map/tan,sbn->tasb/dot_general | solution.py:25
  1264.0 11.7 cholesky.358
  1275.9 9.8 custom-call.31
  1286.4 11.7 cholesky.377
  1298.1 10.3 custom-call.32
  1309.0 11.7 cholesky.398
  1320.8 9.8 custom-call.33
  1331.2 11.7 cholesky.415
  1349.6 6.8 fusion.84
  1356.4 5.2 copy.28
  1361.6 67.4 %all-reduce.10.cloned.1.call-done = f32[512,512]{1,0:T(8,128)} async-done(((f32[512,512]{1,0:T(8,128)}), f32[512,512]{1,0:T(8,128)}) %all-reduce.10.cloned.1.call-update) | async-done | bytes 1048592 | tf_op jit(solution)/shard_map/psum | solution.py:21
  1430.4 8.2 while.9
  1438.6 39.3 %custom-call.34 = f32[4,128,128]{1,2,0:T(8,128)S(1)} custom-call(f32[4,128,128]{2,1,0:T(8,128)S(1)} %get-tuple-element.70), custom_call_target="InvertDiagBlocksLowerTriangular" | custom-call | tf_op jit(solution)/shard_map/jit(_solve_triangular)/triangular_solve | solution.py:58
  1477.9 2.4 fusion.34
  1480.4 3.0 convolution_subtract_fusion.3
  1484.5 3.5 convolution_subtract_fusion.1
  1489.1 5.7 fusion.22
  1496.0 2.5 maximum_bitcast_fusion.1
  1498.4 5.3 copy.29
  1503.8 5.3 copy.30
  1509.1 4.9 select_select_fusion
  1513.9 85.2 %all-reduce.12.cloned.1.call-done = f32[4,512,512]{1,2,0:T(8,128)} async-done(((f32[4,512,512]{1,2,0:T(8,128)}), f32[4,512,512]{1,2,0:T(8,128)}) %all-reduce.12.cloned.1.call-update) | async-done | bytes 4194320 | tf_op jit(solution)/shard_map/psum | solution.py:21
  1603.5 180.4 %collective-permute-done.3 = f32[4,2,512,512]{2,3,0,1:T(8,128)S(1)} collective-permute-done((f32[4,2,512,512]{2,3,0,1:T(8,128)S(1)}, f32[4,2,512,512]{2,3,0,1:T(8,128)S(1)}, u32[]{:S(2)}, u32[]{:S(2)}) %collective-permute-start.3) | collective-permute-done | bytes 8388640 | tf_op jit(solution)/shard_map/ppermute | solution.py:14
  1785.2 3.2 copy-done.2
  1789.9 179.6 %collective-permute-done.4 = f32[4,2,512,512]{2,3,0,1:T(8,128)} collective-permute-done((f32[4,2,512,512]{2,3,0,1:T(8,128)S(1)}, f32[4,2,512,512]{2,3,0,1:T(8,128)}, u32[]{:S(2)}, u32[]{:S(2)}) %collective-permute-start.4) | collective-permute-done | bytes 8388640 | tf_op jit(solution)/shard_map/ppermute | solution.py:14
  1969.5 11.1 add.120
  1983.4 6.8 fusion.4
  1990.2 8.3 fusion
  1998.5 343.2 %collective-permute-done.5 = f32[4,2,512,512]{2,3,0,1:T(8,128)} collective-permute-done((f32[4,2,512,512]{2,3,0,1:T(8,128)}, f32[4,2,512,512]{2,3,0,1:T(8,128)}, u32[]{:S(2)}, u32[]{:S(2)}) %collective-permute-start.5) | collective-permute-done | bytes 8388640 | tf_op jit(solution)/shard_map/ppermute | solution.py:14
  2341.7 11.1 add.121
  2352.8 9.9 copy.32
  2362.7 62.9 %subtract_bitcast_fusion = f32[4,1,512,8,1,512]{2,5,3,0,4,1:T(8,128)} fusion(f32[4,512,8,512]{1,3,2,0:T(8,128)} %fusion, f32[8,512,512,1]{2,1,0,3:T(8,128)} %bitcast.189, f32[4,512,512]{1,2,0:T(8,128)} %all-reduce.12.cloned.1.call-done), kind=kOutput, calls=%fused_computation.4 | convolution fusion | flops 51547996160 | bytes 79691776 | tf_op jit(solution)/shard_map/tan,sbn->tasb/dot_general | solution.py:25
  2425.6 78.2 %copy.35 = f32[4,1,512,8,1,512]{5,4,3,2,1,0:T(1,128)} copy(f32[4,1,512,8,1,512]{2,5,3,0,4,1:T(8,128)} %subtract_bitcast_fusion) | data formatting | bytes 67108864 | tf_op jit(solution)/shard_map/reshape | solution.py:92
  (122 shorter events, 62.4 us)
Async XLA Ops:
  6.5 254.9 %all-reduce.6.cloned.1.call-start = ((), (), s32[]{:S(2)}) async-start(), calls=%async_computation | async-start | bytes 2097152 | tf_op jit(solution)/shard_map/psum | solution.py:21
  172.8 261.4 %all-reduce.8.cloned.1.call-start = ((), (), s32[]{:S(2)}) async-start(), calls=%async_computation.1 | async-start | bytes 8388608 | tf_op jit(solution)/shard_map/psum | solution.py:21
  309.8 6.6 copy-start.4
  345.7 1083.3 %all-reduce.10.cloned.1.call-start = ((), (), s32[]{:S(2)}) async-start(), calls=%async_computation.2 | async-start | bytes 2097152 | tf_op jit(solution)/shard_map/psum | solution.py:21
  434.2 2.2 copy-start
  437.0 181.9 %collective-permute-start = (f32[4,2,512,512]{2,3,0,1:T(8,128)S(1)}, f32[4,2,512,512]{2,3,0,1:T(8,128)S(1)}, u32[]{:S(2)}, u32[]{:S(2)}) collective-permute-start(f32[4,2,512,512]{2,3,0,1:T(8,128)S(1)} %bitcast_dynamic-update-slice_fusion.4), channel_id=1, source_target_pairs={{0,4},{4,0},{8,12},{12,8},{16,20},{20,16},{24,28},{28,24},{1,5},{5... | collective-permute-start | bytes 25165832 | tf_op jit(solution)/shard_map/ppermute | solution.py:14
  620.2 3.2 copy-start.3
  623.4 194.6 %copy-start.6 = (f32[512,512]{1,0:T(8,128)S(1)}, f32[512,512]{1,0:T(8,128)}, u32[]{:S(2)}) copy-start(f32[512,512]{1,0:T(8,128)} %all-reduce.6.cloned.1.call-done) | copy-start | bytes 3145732
  623.4 181.1 %collective-permute-start.1 = (f32[4,2,512,512]{2,3,0,1:T(8,128)S(1)}, f32[4,2,512,512]{2,3,0,1:T(8,128)}, u32[]{:S(2)}, u32[]{:S(2)}) collective-permute-start(f32[4,2,512,512]{2,3,0,1:T(8,128)S(1)} %fusion.8), channel_id=1, source_target_pairs={{0,8},{4,12},{8,0},{12,4},{16,24},{20,28},{24,16},{28,20},{1,9},{5... | collective-permute-start | bytes 25165832 | tf_op jit(solution)/shard_map/ppermute | solution.py:14
  815.6 361.1 %collective-permute-start.2 = (f32[4,2,512,512]{2,3,0,1:T(8,128)}, f32[4,2,512,512]{2,3,0,1:T(8,128)}, u32[]{:S(2)}, u32[]{:S(2)}) collective-permute-start(f32[4,2,512,512]{2,3,0,1:T(8,128)} %add.117), channel_id=1, source_target_pairs={{0,16},{4,20},{8,24},{12,28},{16,0},{20,4},{24,8},{28,12},{1,17},{... | collective-permute-start | bytes 25165832 | tf_op jit(solution)/shard_map/ppermute | solution.py:14
  1349.5 249.6 %all-reduce.12.cloned.1.call-start = ((), (), s32[]{:S(2)}) async-start(), calls=%async_computation.3 | async-start | bytes 8388608 | tf_op jit(solution)/shard_map/psum | solution.py:21
  1477.9 6.6 copy-start.5
  1599.2 2.2 copy-start.1
  1601.9 181.9 %collective-permute-start.3 = (f32[4,2,512,512]{2,3,0,1:T(8,128)S(1)}, f32[4,2,512,512]{2,3,0,1:T(8,128)S(1)}, u32[]{:S(2)}, u32[]{:S(2)}) collective-permute-start(f32[4,2,512,512]{2,3,0,1:T(8,128)S(1)} %bitcast_dynamic-update-slice_fusion.3), channel_id=1, source_target_pairs={{0,4},{4,0},{8,12},{12,8},{16,20},{20,16},{24,28},{28,24},{1,5},{5... | collective-permute-start | bytes 25165832 | tf_op jit(solution)/shard_map/ppermute | solution.py:14
  1785.2 3.2 copy-start.2
  1788.4 194.6 %copy-start.7 = (f32[512,512]{1,0:T(8,128)S(1)}, f32[512,512]{1,0:T(8,128)}, u32[]{:S(2)}) copy-start(f32[512,512]{1,0:T(8,128)} %all-reduce.10.cloned.1.call-done) | copy-start | bytes 3145732
  1788.4 181.1 %collective-permute-start.4 = (f32[4,2,512,512]{2,3,0,1:T(8,128)S(1)}, f32[4,2,512,512]{2,3,0,1:T(8,128)}, u32[]{:S(2)}, u32[]{:S(2)}) collective-permute-start(f32[4,2,512,512]{2,3,0,1:T(8,128)S(1)} %fusion.7), channel_id=1, source_target_pairs={{0,8},{4,12},{8,0},{12,4},{16,24},{20,28},{24,16},{28,20},{1,9},{5... | collective-permute-start | bytes 25165832 | tf_op jit(solution)/shard_map/ppermute | solution.py:14
  1980.6 361.1 %collective-permute-start.5 = (f32[4,2,512,512]{2,3,0,1:T(8,128)}, f32[4,2,512,512]{2,3,0,1:T(8,128)}, u32[]{:S(2)}, u32[]{:S(2)}) collective-permute-start(f32[4,2,512,512]{2,3,0,1:T(8,128)} %add.120), channel_id=1, source_target_pairs={{0,16},{4,20},{8,24},{12,28},{16,0},{20,4},{24,8},{28,12},{1,17},{... | collective-permute-start | bytes 25165832 | tf_op jit(solution)/shard_map/ppermute | solution.py:14
Sparse Core Ops, SparseCore 0:
  172.9 81.0 all-reduce.5
  345.9 88.2 all-reduce.7
  1349.7 79.2 all-reduce.9
  1514.1 85.0 all-reduce.11
